TPU v7x, 256 devices: a whole 4x4x8 slice. The times are simulated.
256 devices in a mesh: grp: 2 (over x_lo), blk: 128 (over x_hi, z, y, core).
Axes of the slice: x: 4 (x_hi: 2, x_lo: 2; x = x_hi * 2 + x_lo), y: 4, z: 8, core: 2. Of those that a mesh axis runs over, the one named last changes fastest.
Arguments:
- atoms: bfloat16 [131072, 512], P(('grp', 'blk')), parts along dimension 0, may hold values from -8 to 8
- edge_mask: int32 [256, 5, 512, 512], P(('grp', 'blk')), parts along dimension 0, may hold values from 0 to 1
- norm_gain: float32 [512], replicated, may hold values from 0.25 to 1.75
- w_query: bfloat16 [512, 512], replicated, may hold values from -3 to 3
- w_key: bfloat16 [512, 512], replicated, may hold values from -3 to 3
- w_value: bfloat16 [512, 512], replicated, may hold values from -0.25 to 0.25
- w_out: bfloat16 [512, 512], replicated, may hold values from -0.25 to 0.25
- bn_gain: float32 [512], replicated, may hold values from 0.25 to 1.75
- bn_shift: float32 [512], replicated, may hold values from -3 to 3
- w_up: bfloat16 [512, 1024], replicated, may hold values from -0.25 to 0.25
- w_down: bfloat16 [1024, 512], replicated, may hold values from -0.1875 to 0.1875
Outputs:
- updated: bfloat16 [131072, 512], P(('grp', 'blk')), parts along dimension 0
There are 2 independent parts, one for each index of `grp`. A program takes and returns all parts, laid end to end along the dimension named above; an argument that names none is the same for every part. Nothing has to cross between parts.
All inputs are finite; a program needn't handle non-finite values.
Results may differ from a plain program's by a relative error of at most 0.01.
The roundings to bfloat16 on the way count: a program that leaves them out, or rounds other values in their place, can miss the bound.
Values may be sent and summed in bfloat16 or wider, within the bound.
A program may use at most 128 MiB of HBM per device.

v0:
```python
import jax
import jax.numpy as jnp
from jax import lax
from jax.sharding import Mesh
from jax.sharding import PartitionSpec as P

D = 512
HEADS = 8
HEAD_DIM = 64
REACH = 2
BLK = ("blk_0", "blk_1", "blk_2", "blk_3")
GRP_BLK = ("grp", "blk_0", "blk_1", "blk_2", "blk_3")


def passed_along(value, axis, steps):
    count = lax.axis_size(axis)
    pairs = [(source, (source + steps) % count) for source in range(count)]
    return lax.ppermute(value, axis, pairs)


def one_axis_at_a_time(value, axes):
    for axis in axes:
        value = lax.psum(value, axis)
    return value


def attend_block(state, query_heads, kv_block, allowed):
    running_top, running_total, running_sum = state
    tile_rows = query_heads.shape[0]
    key_heads = kv_block[0].reshape(tile_rows, HEADS, HEAD_DIM)
    value_heads = kv_block[1].reshape(tile_rows, HEADS, HEAD_DIM)
    score = jnp.einsum(
        "qhd,khd->hqk", query_heads, key_heads, preferred_element_type=jnp.float32
    ) * HEAD_DIM ** (-0.5)
    score = jnp.where(allowed[None], score, -1e30)
    new_top = jnp.maximum(running_top, jnp.max(score, axis=-1))
    factor = jnp.exp(running_top - new_top)
    expo = jnp.exp(score - new_top[:, :, None])
    new_total = running_total * factor + jnp.sum(expo, axis=-1)
    product = jnp.einsum(
        "hqk,khd->qhd", expo.astype(jnp.bfloat16), value_heads, preferred_element_type=jnp.float32
    )
    new_sum = running_sum * jnp.transpose(factor)[:, :, None] + product
    return (new_top, new_total, new_sum)


def project_pair(features, w_key, w_value):
    keys = jnp.dot(features, w_key, preferred_element_type=jnp.float32).astype(jnp.bfloat16)
    values = jnp.dot(features, w_value, preferred_element_type=jnp.float32).astype(jnp.bfloat16)
    return jnp.stack([keys, values])


def body(
    atoms, edge_mask, norm_gain, w_query, w_key, w_value, w_out, bn_gain, bn_shift, w_up, w_down
):
    tile_rows = atoms.shape[0]
    xfull = atoms.astype(jnp.float32)
    normed = (
        xfull * lax.rsqrt(jnp.mean(xfull * xfull, axis=-1, keepdims=True) + 1e-06) * norm_gain
    ).astype(jnp.bfloat16)
    query = jnp.dot(normed, w_query, preferred_element_type=jnp.float32).astype(jnp.bfloat16)
    kv_own = project_pair(normed, w_key, w_value)
    query_heads = query.reshape(tile_rows, HEADS, HEAD_DIM)
    masks = edge_mask[0]
    diagonal = lax.broadcasted_iota(jnp.int32, (tile_rows, tile_rows), 0) == lax.broadcasted_iota(
        jnp.int32, (tile_rows, tile_rows), 1
    )
    state = (
        jnp.full((HEADS, tile_rows), -1e30, jnp.float32),
        jnp.zeros((HEADS, tile_rows), jnp.float32),
        jnp.zeros((tile_rows, HEADS, HEAD_DIM), jnp.float32),
    )
    state = attend_block(state, query_heads, kv_own, (masks[REACH] > 0) | diagonal)
    latest = {1: normed, -1: normed}
    for distance in range(1, REACH + 1):
        for sign in (1, -1):
            offset = sign * distance
            hop = -offset
            received = passed_along(normed, BLK, hop)
            kv_block = project_pair(received, w_key, w_value)
            latest[sign] = received
            state = attend_block(state, query_heads, kv_block, masks[offset + REACH] > 0)
    running_top, running_total, running_sum = state
    mixed = (
        (running_sum / jnp.transpose(running_total)[:, :, None])
        .reshape(tile_rows, D)
        .astype(jnp.bfloat16)
    )
    after = xfull + jnp.dot(mixed, w_out, preferred_element_type=jnp.float32)
    count = tile_rows * lax.axis_size(BLK)
    sums, squares = (
        one_axis_at_a_time(jnp.sum(after, axis=0), BLK),
        one_axis_at_a_time(jnp.sum(after * after, axis=0), BLK),
    )
    mean = sums / count
    var = squares / count - mean * mean
    centered = after - mean
    batched = (centered * lax.rsqrt(var + 1e-05) * bn_gain + bn_shift).astype(jnp.bfloat16)
    hidden = jax.nn.gelu(
        jnp.dot(batched, w_up, preferred_element_type=jnp.float32), approximate=True
    ).astype(jnp.bfloat16)
    return (after + jnp.dot(hidden, w_down, preferred_element_type=jnp.float32)).astype(
        jnp.bfloat16
    )


def solution(mesh):
    torus = Mesh(
        mesh.devices.reshape(mesh.shape["grp"], 2, 8, 4, 2),
        ("grp", "blk_0", "blk_1", "blk_2", "blk_3"),
    )
    return jax.shard_map(
        body,
        mesh=torus,
        in_specs=(
            P(GRP_BLK, None),
            P(GRP_BLK, None, None, None),
            P(),
            P(),
            P(),
            P(),
            P(),
            P(),
            P(),
            P(),
            P(),
        ),
        out_specs=P(GRP_BLK, None),
        check_vma=False,
    )
```

profile of v0, /device:TPU:1, one launch (start us, length us, event | category | flops | bytes accessed | tf_op | source)
XLA Modules:
  0.0 126.8 jit_solution(14850250318351792867)
XLA Ops:
  0.0 0.0 copy-start
  0.0 1.4 %fusion.81 = f32[512]{0:T(512)S(1)} fusion(bf16[512,512]{1,0:T(8,128)(2,1)} %param.11), kind=kLoop, calls=%fused_computation.74 | loop fusion | flops 785920 | bytes 526336 | tf_op jit(solution)/shard_map/reduce_sum | solution.py:59
  1.4 1.6 %fusion.83 = bf16[512,512]{1,0:T(8,128)(2,1)S(1)} fusion(bf16[512,512]{1,0:T(8,128)(2,1)} %param.11, f32[512]{0:T(512)} %param.13, f32[512]{0:T(512)S(1)} %add_rsqrt_fusion.1), kind=kLoop, calls=%fused_computation.76 | loop fusion | flops 1048576 | bytes 1052672 | tf_op jit(solution)/shard_map/convert_element_type | solution.py:60
  3.0 2.2 %collective-permute-start.3 = (bf16[512,512]{1,0:T(8,128)(2,1)S(1)}, bf16[512,512]{1,0:T(8,128)(2,1)}, u32[]{:S(2)}, u32[]{:S(2)}) collective-permute-start(bf16[512,512]{1,0:T(8,128)(2,1)S(1)} %fusion.83), channel_id=1, source_target_pairs={{0,2},{1,3},{2,4},{3,5},{4,6},{5,7},{6,8},{7,9},{8,10},{9,11},{10,... | collective-permute-start | bytes 1572872 | tf_op jit(solution)/shard_map/ppermute | solution.py:18
  5.2 9.3 %collective-permute-start.2 = (bf16[512,512]{1,0:T(8,128)(2,1)S(1)}, bf16[512,512]{1,0:T(8,128)(2,1)}, u32[]{:S(2)}, u32[]{:S(2)}) collective-permute-start(bf16[512,512]{1,0:T(8,128)(2,1)S(1)} %fusion.83), channel_id=1, source_target_pairs={{0,126},{1,127},{2,0},{3,1},{4,2},{5,3},{6,4},{7,5},{8,6},{9,7},{1... | collective-permute-start | bytes 1572872 | tf_op jit(solution)/shard_map/ppermute | solution.py:18
  14.5 0.0 collective-permute-start.1
  14.5 1.0 collective-permute-start
  15.5 2.3 %convolution_convert_fusion.8 = bf16[512,512]{0,1:T(8,128)(2,1)} fusion(bf16[512,512]{1,0:T(8,128)(2,1)S(1)} %fusion.83, bf16[512,512]{1,0:T(8,128)(2,1)} %param.16), kind=kOutput, calls=%fused_computation.71 | convolution fusion | flops 268697600 | bytes 1572864 | tf_op jit(solution)/shard_map/dot_general | solution.py:49
  17.8 2.3 %convolution_convert_fusion.9 = bf16[512,512]{0,1:T(8,128)(2,1)} fusion(bf16[512,512]{1,0:T(8,128)(2,1)S(1)} %fusion.83, bf16[512,512]{1,0:T(8,128)(2,1)} %param.15), kind=kOutput, calls=%fused_computation.72 | convolution fusion | flops 268697600 | bytes 1572864 | tf_op jit(solution)/shard_map/dot_general | solution.py:48
  20.1 1.5 %convolution_convert_fusion.10 = bf16[512,512]{0,1:T(8,128)(2,1)S(1)} fusion(bf16[512,512]{1,0:T(8,128)(2,1)S(1)} %fusion.83, bf16[512,512]{1,0:T(8,128)(2,1)} %param.14), kind=kOutput, calls=%fused_computation.73 | convolution fusion | flops 268697600 | bytes 1572864 | tf_op jit(solution)/shard_map/dot_general | solution.py:61
  21.6 0.0 copy-done.3
  21.7 0.0 copy-start.1
  21.7 1.4 %fusion.91 = (pred[512,512]{1,0:T(8,128)(4,1)S(1)}, pred[512,512]{1,0:T(8,128)(4,1)}, pred[512,512]{1,0:T(8,128)(4,1)S(1)}, pred[512,512]{1,0:T(8,128)(4,1)}) fusion(s32[1,5,512,512]{3,2,1,0:T(8,128)S(1)} %copy-done.3), kind=kLoop, calls=%fused_computation.92 | loop fusion | flops 1048576 | bytes 5242880 | tf_op jit(solution)/shard_map/gt | solution.py:82
  23.0 0.2 fusion.89
  23.2 1.0 copy.12
  24.3 0.4 copy.16
  24.7 1.3 %copy.14 = pred[512,512]{0,1:T(8,128)(4,1)S(1)} copy(pred[512,512]{1,0:T(8,128)(4,1)} %get-tuple-element.24) | data formatting | bytes 524288 | tf_op jit(solution)/shard_map/gt | solution.py:82
  26.0 1.1 copy.20
  27.1 1.3 %copy.18 = pred[512,512]{0,1:T(8,128)(4,1)S(1)} copy(pred[512,512]{1,0:T(8,128)(4,1)} %get-tuple-element.26) | data formatting | bytes 524288 | tf_op jit(solution)/shard_map/gt | solution.py:82
  28.4 2.6 %fusion = (f32[8,512]{1,0:T(8,128)S(1)}, f32[8,512,512]{1,2,0:T(8,128)S(1)}) fusion(pred[512,512]{0,1:T(8,128)(4,1)} %copy.12, bf16[512,8,64]{0,2,1:T(8,128)(2,1)S(1)} %bitcast.193, bf16[512,8,64]{0,2,1:T(8,128)(2,1)} %bitcast.198), kind=kOutput, calls=%fused_computation.10 | convolution fusion | flops 274722816 | bytes 9715712 | tf_op jit(solution)/shard_map/qhd,khd->hqk/dot_general | solution.py:32
  31.0 0.0 copy-start.5
  31.0 0.0 collective-permute-done.2
  31.0 0.0 copy-done.1
  31.0 1.6 %convolution_convert_fusion.3 = bf16[512,512]{0,1:T(8,128)(2,1)S(1)} fusion(bf16[512,512]{1,0:T(8,128)(2,1)} %collective-permute-done.2, bf16[512,512]{1,0:T(8,128)(2,1)S(1)} %copy-done.1), kind=kOutput, calls=%fused_computation.66 | convolution fusion | flops 268697600 | bytes 1572864 | tf_op jit(solution)/shard_map/dot_general | solution.py:48
  32.6 1.5 %fusion.3 = (f32[8,512]{1,0:T(8,128)S(1)}, f32[8,512,512]{1,2,0:T(8,128)S(1)}) fusion(pred[512,512]{0,1:T(8,128)(4,1)S(1)} %copy.18, bf16[512,8,64]{0,2,1:T(8,128)(2,1)S(1)} %bitcast.194, bf16[512,8,64]{0,2,1:T(8,128)(2,1)S(1)} %bitcast.200), kind=kOutput, calls=%fused_computation.13 | convolution fusion | flops 274722816 | bytes 9715712 | tf_op jit(solution)/shard_map/qhd,khd->hqk/dot_general | solution.py:32
  34.1 0.0 collective-permute-done.3
  34.1 1.5 %convolution_convert_fusion.1 = bf16[512,512]{0,1:T(8,128)(2,1)S(1)} fusion(bf16[512,512]{1,0:T(8,128)(2,1)} %collective-permute-done.3, bf16[512,512]{1,0:T(8,128)(2,1)S(1)} %copy-done.1), kind=kOutput, calls=%fused_computation.64 | convolution fusion | flops 268697600 | bytes 1572864 | tf_op jit(solution)/shard_map/dot_general | solution.py:48
  35.7 0.0 copy-done.5
  35.7 1.5 %fusion.4 = (f32[8,512]{1,0:T(8,128)S(1)}, f32[8,512,512]{1,2,0:T(8,128)S(1)}) fusion(pred[512,512]{0,1:T(8,128)(4,1)S(1)} %copy-done.5, bf16[512,8,64]{0,2,1:T(8,128)(2,1)S(1)} %bitcast.195, bf16[512,8,64]{0,2,1:T(8,128)(2,1)S(1)} %bitcast.201), kind=kOutput, calls=%fused_computation.14 | convolution fusion | flops 274722816 | bytes 9715712 | tf_op jit(solution)/shard_map/qhd,khd->hqk/dot_general | solution.py:32
  37.2 0.0 collective-permute-done
  37.2 1.5 %convolution_convert_fusion.7 = bf16[512,512]{0,1:T(8,128)(2,1)S(1)} fusion(bf16[512,512]{1,0:T(8,128)(2,1)} %collective-permute-done, bf16[512,512]{1,0:T(8,128)(2,1)S(1)} %copy-done.1), kind=kOutput, calls=%fused_computation.70 | convolution fusion | flops 268697600 | bytes 1572864 | tf_op jit(solution)/shard_map/dot_general | solution.py:48
  38.7 4.7 %fusion.1 = (f32[8,512]{1,0:T(8,128)S(1)}, f32[8,512,512]{1,2,0:T(8,128)}) fusion(pred[512,512]{0,1:T(8,128)(4,1)S(1)} %copy.14, bf16[512,8,64]{0,2,1:T(8,128)(2,1)S(1)} %bitcast.196, bf16[512,8,64]{0,2,1:T(8,128)(2,1)S(1)} %bitcast.202), kind=kOutput, calls=%fused_computation.11 | convolution fusion | flops 274722816 | bytes 9715712 | tf_op jit(solution)/shard_map/qhd,khd->hqk/dot_general | solution.py:32
  43.4 0.0 collective-permute-done.1
  43.4 1.5 %convolution_convert_fusion.5 = bf16[512,512]{0,1:T(8,128)(2,1)S(1)} fusion(bf16[512,512]{1,0:T(8,128)(2,1)} %collective-permute-done.1, bf16[512,512]{1,0:T(8,128)(2,1)S(1)} %copy-done.1), kind=kOutput, calls=%fused_computation.68 | convolution fusion | flops 268697600 | bytes 1572864 | tf_op jit(solution)/shard_map/dot_general | solution.py:48
  44.9 4.9 %fusion.2 = (f32[8,512]{1,0:T(8,128)S(1)}, f32[8,512,512]{1,2,0:T(8,128)}) fusion(pred[512,512]{0,1:T(8,128)(4,1)S(1)} %copy.16, bf16[512,8,64]{0,2,1:T(8,128)(2,1)S(1)} %bitcast.197, bf16[512,8,64]{0,2,1:T(8,128)(2,1)S(1)} %bitcast.199), kind=kOutput, calls=%fused_computation.12 | convolution fusion | flops 274722816 | bytes 9715712 | tf_op jit(solution)/shard_map/qhd,khd->hqk/dot_general | solution.py:32
  49.9 2.7 %fusion.13 = f32[8,512]{1,0:T(8,128)S(1)} fusion(f32[8,512,512]{1,2,0:T(8,128)S(1)} %get-tuple-element.33, f32[8,512]{1,0:T(8,128)S(1)} %get-tuple-element.19, pred[512,512]{0,1:T(8,128)(4,1)} %copy.20), kind=kLoop, calls=%fused_computation.23 | loop fusion | flops 8384512 | bytes 8683520 | tf_op jit(solution)/shard_map/reduce_sum | solution.py:39
  52.6 5.7 %fusion.9 = (f32[8,512]{1,0:T(8,128)S(1)}, f32[8,512]{1,0:T(8,128)S(1)}) fusion(f32[8,512,512]{1,2,0:T(8,128)} %get-tuple-element.37, f32[8,512]{1,0:T(8,128)S(1)} %get-tuple-element.21, pred[512,512]{0,1:T(8,128)(4,1)S(1)} %copy.16, f32[8,512]{1,0:T(8,128)S(1)} %get-tuple-element.20, f32[8,512,512]{1,2,0:T(8,128)S(1)} %get-tuple-element.35, ...), kind=kLoop, calls=%fused_computation.19 | loop fusion | flops 16769024 | bytes 17367040 | tf_op jit(solution)/shard_map/reduce_sum | solution.py:39
  58.3 0.0 copy-start.8
  58.3 5.7 %fusion.5 = (f32[8,512]{1,0:T(8,128)S(1)}, f32[8,512]{1,0:T(8,128)S(1)}) fusion(f32[8,512,512]{1,2,0:T(8,128)S(1)} %get-tuple-element.41, f32[8,512]{1,0:T(8,128)S(1)} %get-tuple-element.29, pred[512,512]{0,1:T(8,128)(4,1)S(1)} %copy-done.4, f32[8,512]{1,0:T(8,128)S(1)} %get-tuple-element.22, f32[8,512,512]{1,2,0:T(8,128)} %get-tuple-element.39, ...), kind=kLoop, calls=%fused_computation.15 | loop fusion | flops 16769024 | bytes 17367040 | tf_op jit(solution)/shard_map/reduce_sum | solution.py:39
  64.1 0.0 copy-start.2
  64.1 2.3 %fusion.68 = f32[512,8,64]{0,2,1:T(8,128)S(1)} fusion(bf16[512,8,64]{0,2,1:T(8,128)(2,1)S(1)} %bitcast.203, f32[8,512,512]{1,2,0:T(8,128)S(1)} %get-tuple-element.41, f32[8,512]{1,0:T(8,128)S(1)} %get-tuple-element.29, pred[512,512]{0,1:T(8,128)(4,1)S(1)} %copy-done.4, f32[512,8]{0,1:T(8,128)S(1)} %get-tuple-element.27, f32[512,8]{0,1:T(8,128)S(1)} %get-tuple-element.28), kind=kOutput, calls=%fused_computation.58 | convolution fusion | flops 277348352 | bytes 10272768 | tf_op jit(solution)/shard_map/hqk,khd->qhd/dot_general | solution.py:40
  66.5 0.0 slice-start
  66.5 1.7 %convolution_convert_fusion.6 = bf16[512,512]{0,1:T(8,128)(2,1)S(1)} fusion(bf16[512,512]{1,0:T(8,128)(2,1)} %collective-permute-done, bf16[512,512]{1,0:T(8,128)(2,1)S(1)} %copy-done.2), kind=kOutput, calls=%fused_computation.69 | convolution fusion | flops 268697600 | bytes 1572864 | tf_op jit(solution)/shard_map/dot_general | solution.py:49
  68.1 0.0 slice-start.1
  68.2 5.8 %fusion.71 = f32[512,8,64]{0,2,1:T(8,128)S(1)} fusion(f32[512,8,64]{0,2,1:T(8,128)S(1)} %fusion.68, bf16[512,8,64]{0,2,1:T(8,128)(2,1)S(1)} %bitcast.205, f32[8,512,512]{1,2,0:T(8,128)} %get-tuple-element.39, f32[8,512]{1,0:T(8,128)S(1)} %get-tuple-element.22, pred[512,512]{0,1:T(8,128)(4,1)S(1)} %copy.14, f32[512,8]{0,1:T(8,128)S(1)} %get-tuple-element.18), kind=kOutput, calls=%fused_computation.59 | convolution fusion | flops 277348352 | bytes 11304960 | tf_op jit(solution)/shard_map/hqk,khd->qhd/dot_general | solution.py:40
  73.9 1.5 %convolution_convert_fusion.4 = bf16[512,512]{0,1:T(8,128)(2,1)S(1)} fusion(bf16[512,512]{1,0:T(8,128)(2,1)} %collective-permute-done.1, bf16[512,512]{1,0:T(8,128)(2,1)S(1)} %copy-done.2), kind=kOutput, calls=%fused_computation.67 | convolution fusion | flops 268697600 | bytes 1572864 | tf_op jit(solution)/shard_map/dot_general | solution.py:49
  75.5 2.3 %fusion.74 = f32[512,8,64]{0,2,1:T(8,128)S(1)} fusion(f32[512,8,64]{0,2,1:T(8,128)S(1)} %fusion.71, bf16[512,8,64]{0,2,1:T(8,128)(2,1)S(1)} %bitcast.206, f32[8,512,512]{1,2,0:T(8,128)S(1)} %bitcast.192, f32[8,512]{1,0:T(8,128)S(1)} %get-tuple-element.21, pred[512,512]{0,1:T(8,128)(4,1)S(1)} %copy.16, f32[512,8]{0,1:T(8,128)S(1)} %get-tuple-element.17), kind=kOutput, calls=%fused_computation.60 | convolution fusion | flops 277348352 | bytes 11304960 | tf_op jit(solution)/shard_map/hqk,khd->qhd/dot_general | solution.py:40
  77.8 1.6 %convolution_convert_fusion.2 = bf16[512,512]{0,1:T(8,128)(2,1)S(1)} fusion(bf16[512,512]{1,0:T(8,128)(2,1)} %collective-permute-done.2, bf16[512,512]{1,0:T(8,128)(2,1)S(1)} %copy-done.2), kind=kOutput, calls=%fused_computation.65 | convolution fusion | flops 268697600 | bytes 1572864 | tf_op jit(solution)/shard_map/dot_general | solution.py:49
  79.4 2.6 %fusion.77 = f32[512,8,64]{0,2,1:T(8,128)S(1)} fusion(f32[512,8,64]{0,2,1:T(8,128)S(1)} %fusion.74, bf16[512,8,64]{0,2,1:T(8,128)(2,1)S(1)} %bitcast.207, f32[8,512,512]{1,2,0:T(8,128)S(1)} %get-tuple-element.35, f32[8,512]{1,0:T(8,128)S(1)} %get-tuple-element.20, pred[512,512]{0,1:T(8,128)(4,1)S(1)} %copy.18, f32[512,8]{0,1:T(8,128)S(1)} %get-tuple-element.16), kind=kOutput, calls=%fused_computation.61 | convolution fusion | flops 277348352 | bytes 11304960 | tf_op jit(solution)/shard_map/hqk,khd->qhd/dot_general | solution.py:40
  82.0 0.0 copy-start.7
  82.0 0.0 copy-start.10
  82.0 1.6 %convolution_convert_fusion = bf16[512,512]{0,1:T(8,128)(2,1)S(1)} fusion(bf16[512,512]{1,0:T(8,128)(2,1)} %collective-permute-done.3, bf16[512,512]{1,0:T(8,128)(2,1)S(1)} %copy-done.2), kind=kOutput, calls=%fused_computation.63 | convolution fusion | flops 268697600 | bytes 1572864 | tf_op jit(solution)/shard_map/dot_general | solution.py:49
  83.6 0.0 copy-start.9
  83.6 0.0 copy-start.11
  83.7 0.0 copy-start.12
  83.7 2.4 %divide_convert_fusion = bf16[512,8,64]{0,2,1:T(8,128)(2,1)S(1)} fusion(f32[512,8,64]{0,2,1:T(8,128)S(1)} %fusion.77, bf16[512,8,64]{0,2,1:T(8,128)(2,1)S(1)} %bitcast.204, f32[8,512,512]{1,2,0:T(8,128)S(1)} %get-tuple-element.33, f32[8,512]{1,0:T(8,128)S(1)} %get-tuple-element.19, pred[512,512]{0,1:T(8,128)(4,1)S(1)} %copy-done.6, ...), kind=kOutput, calls=%fused_computation.82 | convolution fusion | flops 277610496 | bytes 10780672 | tf_op jit(solution)/shard_map/hqk,khd->qhd/dot_general | solution.py:40
  86.1 0.5 fusion.128
  86.6 5.3 %all-reduce.3 = (f32[512]{0:T(512)S(1)}, f32[512]{0:T(512)S(1)}) all-reduce(f32[512]{0:T(512)S(1)} %get-tuple-element.6, f32[512]{0:T(512)S(1)} %get-tuple-element.5), channel_id=1, replica_groups=mesh['grp'=2,'blk_0'=2,'blk_1'=8,'blk_2'=4,'blk_3'=2] {'blk_0'}, use_global_device_ids=true, to_apply=%region_17.18 | all-reduce | flops 1024 | bytes 8192 | tf_op jit(solution)/shard_map/psum | solution.py:23
  91.9 10.7 %all-reduce = (f32[512]{0:T(512)S(1)}, f32[512]{0:T(512)S(1)}) all-reduce(f32[512]{0:T(512)S(1)} %get-tuple-element.13, f32[512]{0:T(512)S(1)} %get-tuple-element.14), channel_id=1, replica_groups=mesh['grp'=2,'blk_0'=2,'blk_1'=8,'blk_2'=4,'blk_3'=2] {'blk_1'}, use_global_device_ids=true, to_apply=%region_18.19 | all-reduce | flops 1024 | bytes 8192 | tf_op jit(solution)/shard_map/psum | solution.py:23
  102.6 11.0 %all-reduce.1 = (f32[512]{0:T(512)S(1)}, f32[512]{0:T(512)S(1)}) all-reduce(f32[512]{0:T(512)S(1)} %get-tuple-element.7, f32[512]{0:T(512)S(1)} %get-tuple-element.8), channel_id=1, replica_groups=mesh['grp'=2,'blk_0'=2,'blk_1'=8,'blk_2'=4,'blk_3'=2] {'blk_2'}, use_global_device_ids=true, to_apply=%region_19.20 | all-reduce | flops 1024 | bytes 8192 | tf_op jit(solution)/shard_map/psum | solution.py:23
  113.6 10.9 %all-reduce.2 = (f32[512]{0:T(512)S(1)}, f32[512]{0:T(512)S(1)}) all-reduce(f32[512]{0:T(512)S(1)} %get-tuple-element.9, f32[512]{0:T(512)S(1)} %get-tuple-element.10), channel_id=1, replica_groups=mesh['grp'=2,'blk_0'=2,'blk_1'=8,'blk_2'=4,'blk_3'=2] {'blk_3'}, use_global_device_ids=true, to_apply=%region_20.21 | all-reduce | flops 1024 | bytes 8192 | tf_op jit(solution)/shard_map/psum | solution.py:23
  124.5 0.0 copy-done.11
  124.5 0.0 copy-done.12
  124.5 2.2 %fusion.80 = bf16[512,512]{1,0:T(8,128)(2,1)} fusion(f32[512,512]{1,0:T(8,128)S(1)} %get-tuple-element.42, bf16[1024,512]{1,0:T(8,128)(2,1)S(1)} %copy-done, bf16[512,1024]{1,0:T(8,128)(2,1)S(1)} %copy-done.9, f32[512]{0:T(512)S(1)} %copy-done.11, f32[512]{0:T(512)S(1)} %copy-done.12, f32[512]{0:T(512)S(1)} %get-tuple-element.31, f32[512]{0:T(512)S(1)} %get-tuple-element.30), kind=kOutput, calls=%fused_computation.62 | convolution fusion | flops 1080295424 | bytes 3678208 | tf_op jit(solution)/shard_map/dot_general | solution.py:102
  (18 shorter events, 0.1 us)
Async XLA Ops:
  0.0 124.5 %copy-start = (bf16[1024,512]{1,0:T(8,128)(2,1)S(1)}, bf16[1024,512]{1,0:T(8,128)(2,1)}, u32[]{:S(2)}) copy-start(bf16[1024,512]{1,0:T(8,128)(2,1)} %param.21) | copy-start | bytes 3145732
  0.0 21.6 %copy-start.3 = (s32[1,5,512,512]{3,2,1,0:T(8,128)S(1)}, s32[1,5,512,512]{3,2,1,0:T(8,128)}, u32[]{:S(2)}) copy-start(s32[1,5,512,512]{3,2,1,0:T(8,128)} %param.12) | copy-start | bytes 15728644
  3.0 31.1 %collective-permute-start.3 = (bf16[512,512]{1,0:T(8,128)(2,1)S(1)}, bf16[512,512]{1,0:T(8,128)(2,1)}, u32[]{:S(2)}, u32[]{:S(2)}) collective-permute-start(bf16[512,512]{1,0:T(8,128)(2,1)S(1)} %fusion.83), channel_id=1, source_target_pairs={{0,2},{1,3},{2,4},{3,5},{4,6},{5,7},{6,8},{7,9},{8,10},{9,11},{10,... | collective-permute-start | bytes 1572872 | tf_op jit(solution)/shard_map/ppermute | solution.py:18
  5.2 25.8 %collective-permute-start.2 = (bf16[512,512]{1,0:T(8,128)(2,1)S(1)}, bf16[512,512]{1,0:T(8,128)(2,1)}, u32[]{:S(2)}, u32[]{:S(2)}) collective-permute-start(bf16[512,512]{1,0:T(8,128)(2,1)S(1)} %fusion.83), channel_id=1, source_target_pairs={{0,126},{1,127},{2,0},{3,1},{4,2},{5,3},{6,4},{7,5},{8,6},{9,7},{1... | collective-permute-start | bytes 1572872 | tf_op jit(solution)/shard_map/ppermute | solution.py:18
  14.5 28.9 %collective-permute-start.1 = (bf16[512,512]{1,0:T(8,128)(2,1)S(1)}, bf16[512,512]{1,0:T(8,128)(2,1)}, u32[]{:S(2)}, u32[]{:S(2)}) collective-permute-start(bf16[512,512]{1,0:T(8,128)(2,1)S(1)} %fusion.83), channel_id=1, source_target_pairs={{0,1},{1,2},{2,3},{3,4},{4,5},{5,6},{6,7},{7,8},{8,9},{9,10},{10,1... | collective-permute-start | bytes 1572872 | tf_op jit(solution)/shard_map/ppermute | solution.py:18
  14.5 22.7 %collective-permute-start = (bf16[512,512]{1,0:T(8,128)(2,1)S(1)}, bf16[512,512]{1,0:T(8,128)(2,1)}, u32[]{:S(2)}, u32[]{:S(2)}) collective-permute-start(bf16[512,512]{1,0:T(8,128)(2,1)S(1)} %fusion.83), channel_id=1, source_target_pairs={{0,127},{1,0},{2,1},{3,2},{4,3},{5,4},{6,5},{7,6},{8,7},{9,8},{10,... | collective-permute-start | bytes 1572872 | tf_op jit(solution)/shard_map/ppermute | solution.py:18
  21.7 9.4 %copy-start.1 = (bf16[512,512]{1,0:T(8,128)(2,1)S(1)}, bf16[512,512]{1,0:T(8,128)(2,1)}, u32[]{:S(2)}) copy-start(bf16[512,512]{1,0:T(8,128)(2,1)} %param.15) | copy-start | bytes 1572868
  31.0 4.7 %copy-start.5 = (pred[512,512]{0,1:T(8,128)(4,1)S(1)}, pred[512,512]{0,1:T(8,128)(4,1)}, u32[]{:S(2)}) copy-start(pred[512,512]{0,1:T(8,128)(4,1)} %copy.20) | copy-start | bytes 786436
  52.6 5.7 %copy-start.4 = (pred[512,512]{0,1:T(8,128)(4,1)S(1)}, pred[512,512]{0,1:T(8,128)(4,1)}, u32[]{:S(2)}) copy-start(pred[512,512]{0,1:T(8,128)(4,1)} %copy.12) | copy-start | bytes 786436
  58.3 5.8 %copy-start.8 = (bf16[512,512]{0,1:T(8,128)(2,1)S(1)}, bf16[512,512]{0,1:T(8,128)(2,1)}, u32[]{:S(2)}) copy-start(bf16[512,512]{0,1:T(8,128)(2,1)} %convolution_convert_fusion.8) | copy-start | bytes 1572868
  64.1 2.4 %copy-start.2 = (bf16[512,512]{1,0:T(8,128)(2,1)S(1)}, bf16[512,512]{1,0:T(8,128)(2,1)}, u32[]{:S(2)}) copy-start(bf16[512,512]{1,0:T(8,128)(2,1)} %param.16) | copy-start | bytes 1572868
  66.5 9.0 %slice-start = ((s8[8388608]{0:T(1024)(128)(4,1)}), s8[4194304]{0:T(1024)(128)(4,1)S(1)}, s32[]{:S(2)}) async-start(s8[8388608]{0:T(1024)(128)(4,1)} %bitcast.191), calls=%async_computation | async-start | bytes 8388608
  68.1 7.3 %slice-start.1 = ((s8[8388608]{0:T(1024)(128)(4,1)}), s8[4194304]{0:T(1024)(128)(4,1)S(1)}, s32[]{:S(2)}) async-start(s8[8388608]{0:T(1024)(128)(4,1)} %bitcast.191), calls=%async_computation.1 | async-start | bytes 8388608
  77.8 5.8 %copy-start.6 = (pred[512,512]{0,1:T(8,128)(4,1)S(1)}, pred[512,512]{0,1:T(8,128)(4,1)}, u32[]{:S(2)}) copy-start(pred[512,512]{0,1:T(8,128)(4,1)} %copy.20) | copy-start | bytes 786436
  82.0 4.1 %copy-start.7 = (bf16[512,512]{1,0:T(8,128)(2,1)S(1)}, bf16[512,512]{1,0:T(8,128)(2,1)}, u32[]{:S(2)}) copy-start(bf16[512,512]{1,0:T(8,128)(2,1)} %param.11) | copy-start | bytes 1572868
  82.0 4.1 %copy-start.10 = (bf16[512,512]{1,0:T(8,128)(2,1)S(1)}, bf16[512,512]{1,0:T(8,128)(2,1)}, u32[]{:S(2)}) copy-start(bf16[512,512]{1,0:T(8,128)(2,1)} %param.17) | copy-start | bytes 1572868
  83.6 40.9 %copy-start.9 = (bf16[512,1024]{1,0:T(8,128)(2,1)S(1)}, bf16[512,1024]{1,0:T(8,128)(2,1)}, u32[]{:S(2)}) copy-start(bf16[512,1024]{1,0:T(8,128)(2,1)} %param.20) | copy-start | bytes 3145732
  83.6 40.9 %copy-start.11 = (f32[512]{0:T(512)S(1)}, f32[512]{0:T(512)}, u32[]{:S(2)}) copy-start(f32[512]{0:T(512)} %param.19) | copy-start | bytes 6148
  83.7 40.9 %copy-start.12 = (f32[512]{0:T(512)S(1)}, f32[512]{0:T(512)}, u32[]{:S(2)}) copy-start(f32[512]{0:T(512)} %param.18) | copy-start | bytes 6148
where the time goes:
time: 127 us
  matrix products  52 us (41%)
  blocking collectives  37.9 us (30%)
  other arithmetic  18.7 us (15%)
  starting transfers between devices  12.4 us (10%)
  local copies, waits for them, and re-layouts  5.27 us (4%)
    psum x4, blocking collectives, one_axis_at_a_time(): value = lax.psum(value, axis)  37.9 us
    dot_general x5, matrix products, attend_block(): jnp.einsum('hqk,khd->qhd', expo.astype(jnp.bfloat16), value_heads, prefer...  15.4 us
    dot_general x5, matrix products, attend_block(): jnp.einsum('qhd,khd->hqk', query_heads, key_heads, preferred_element_type...  15.2 us
    reduce_sum x3, other arithmetic, attend_block(): new_total = running_total * factor + jnp.sum(expo, axis=-1)  14.1 us
    ppermute x4, starting transfers between devices, passed_along(): return lax.ppermute(value, axis, pairs)  12.4 us
    dot_general x5, matrix products, project_pair(): jnp.dot(features, w_value, preferred_element_type=jnp.float32)  8.7 us
    dot_general x5, matrix products, project_pair(): jnp.dot(features, w_key, preferred_element_type=jnp.float32)  8.45 us
    gt x4, local copies, waits for them, and re-layouts, body(): masks[offset + REACH] > 0  4.14 us
  transfers between devices with their start and end apart: 4, of which 0 were waited for; matrix products, arithmetic and copies ran while one was open for 22% of the time, Pallas kernels for 0%

commit v1 on v0

v1 whole, which is shorter than its diff:
```python
import functools
import math

import jax
import jax.numpy as jnp
from jax import lax
from jax.experimental import pallas as pl
from jax.experimental.pallas import tpu as pltpu
from jax.sharding import PartitionSpec as P

F32 = jnp.float32
BF16 = jnp.bfloat16
T = 512
D = 512
HEADS = 8
HEAD_DIM = 64
FF = 1024
SLABS = 5
VROWS = 80
AROWS = 72
CHUNKS = 2
CROWS = T // CHUNKS
NEG = -1e30
SCALE = HEAD_DIM**-0.5 * math.log2(math.e)
NY, NZ, NX = 4, 8, 2
PLANE = NX * NY * 2
BLOCKS = PLANE * NZ


def mm(a, b):
    return jnp.dot(a, b, preferred_element_type=F32)


def mm_nt(a, b):
    return lax.dot_general(a, b, (((1,), (1,)), ((), ())), preferred_element_type=F32)


def kernel(
    atoms_hbm, mask_hbm, gain_hbm, wq_hbm, wk_hbm, wv_hbm, wo_hbm, bng_hbm, bns_hbm, wu_hbm, wd_hbm,
    out_hbm,
    atoms, mask, gain, wq, wk, wv, wo, bng, bns, wu, wd,
    nrm, recv, wqt, wvt, qz, keys, vals, bias, t0, t1, p0, p1, a0, a1, top, acc,
    mixed, after, result, stat, stat_a, stat_m, stat_b,
    load_sem, out_sem, own_send, own_recv, fst_send, fst_recv, fwd_send, fwd_recv, snd_send, snd_recv,
    sa_send, sa_recv, sb_send, sb_recv,
):
    me = lax.axis_index("blk")
    core = lax.rem(me, 2)
    y = lax.rem(me // 2, NY)
    z = lax.rem(me // (2 * NY), NZ)
    xh = me // (2 * NY * NZ)
    sgn = 1 - 2 * core
    partner = me + sgn
    ahead = lax.rem(me + 2 * sgn + BLOCKS, BLOCKS)
    behind = lax.rem(me - 2 * sgn + BLOCKS, BLOCKS)
    place = xh * (NY * 2) + y * 2 + core

    def plane_peer(j):
        u = lax.rem(place + j, PLANE)
        return ((u // (NY * 2)) * NZ + z) * (NY * 2) + lax.rem(u, NY * 2)

    def line_peer(j):
        return (xh * NZ + lax.rem(z + j, NZ)) * (NY * 2) + y * 2 + core

    offsets = [2, 2 + sgn, 2 + 2 * sgn, 2 - sgn, 2 - 2 * sgn]
    loads = [
        pltpu.make_async_copy(atoms_hbm, atoms, load_sem.at[0]),
        pltpu.make_async_copy(gain_hbm, gain, load_sem.at[1]),
        pltpu.make_async_copy(wq_hbm, wq, load_sem.at[2]),
        pltpu.make_async_copy(wk_hbm, wk, load_sem.at[3]),
        pltpu.make_async_copy(wv_hbm, wv, load_sem.at[4]),
    ]
    mask_loads = [
        pltpu.make_async_copy(mask_hbm.at[0, offsets[s]], mask.at[s], load_sem.at[5 + s])
        for s in range(SLABS)
    ]
    late = [
        pltpu.make_async_copy(wo_hbm, wo, load_sem.at[10]),
        pltpu.make_async_copy(bng_hbm, bng, load_sem.at[11]),
        pltpu.make_async_copy(bns_hbm, bns, load_sem.at[12]),
        pltpu.make_async_copy(wu_hbm, wu, load_sem.at[13]),
        pltpu.make_async_copy(wd_hbm, wd, load_sem.at[14]),
    ]
    for copy in loads + mask_loads + late:
        copy.start()

    barrier = pltpu.get_barrier_semaphore()
    peers = [partner, ahead, behind]
    peers += [plane_peer(j) for j in range(1, PLANE)]
    peers += [line_peer(j) for j in range(1, NZ)]
    for peer in peers:
        pl.semaphore_signal(
            barrier, inc=1, device_id={"blk": peer}, device_id_type=pl.DeviceIdType.MESH
        )

    def remote(src, dst, send, rec, device):
        return pltpu.make_async_remote_copy(
            src_ref=src, dst_ref=dst, send_sem=send, recv_sem=rec,
            device_id={"blk": device}, device_id_type=pl.DeviceIdType.MESH,
        )

    def rows(c):
        return pl.ds(c * CROWS, CROWS)

    own = remote(nrm, recv.at[0], own_send, own_recv, partner)
    first = [
        remote(nrm.at[rows(c)], recv.at[1, rows(c)], fst_send.at[c], fst_recv.at[c], behind)
        for c in range(CHUNKS)
    ]
    passed = [
        remote(recv.at[1, rows(c)], recv.at[2, rows(c)], fwd_send.at[c], fwd_recv.at[c], partner)
        for c in range(CHUNKS)
    ]
    second = [
        remote(nrm.at[rows(c)], recv.at[3, rows(c)], snd_send.at[c], snd_recv.at[c], ahead)
        for c in range(CHUNKS)
    ]

    loads[0].wait()
    loads[1].wait()
    x = atoms[...].astype(F32)
    nrm[...] = (
        x * lax.rsqrt(jnp.mean(x * x, axis=-1, keepdims=True) + 1e-6) * gain[...]
    ).astype(BF16)
    pl.semaphore_wait(barrier, len(peers))
    for copy in first:
        copy.start()
    own.start()

    for copy in loads[2:]:
        copy.wait()
    wqt[...] = wq[...].T
    wvt[...] = wv[...].T

    def project(slot, features):
        k = mm(features, wk[...]).astype(BF16)
        for pair in range(HEADS // 2):
            keys[slot, pair] = k[:, pair * 128 : (pair + 1) * 128]
        v = mm_nt(wvt[...], features).astype(BF16)
        for h in range(HEADS):
            vals[slot, h, 0:HEAD_DIM] = v[h * HEAD_DIM : (h + 1) * HEAD_DIM]

    def make_bias(slot):
        mask_loads[slot].wait()
        for kc in range(T // 128):
            allowed = mask[slot, :, kc * 128 : (kc + 1) * 128] > 0
            if slot == 0:
                r = lax.broadcasted_iota(jnp.int32, (T, 128), 0)
                c = lax.broadcasted_iota(jnp.int32, (T, 128), 1) + kc * 128
                allowed = allowed | (r == c)
            bias[slot, kc * 128 : (kc + 1) * 128] = jnp.where(allowed, 0.0, NEG).astype(F32).T

    features = nrm[...]
    q = mm_nt(wqt[...], features).astype(BF16)
    zero = jnp.zeros((HEAD_DIM, T), BF16)
    for h in range(HEADS):
        part = q[h * HEAD_DIM : (h + 1) * HEAD_DIM]
        qz[h, 0:HEAD_DIM] = part if h % 2 == 0 else zero
        qz[h, HEAD_DIM : 2 * HEAD_DIM] = zero if h % 2 == 0 else part
    for s in range(SLABS):
        for h in range(HEADS):
            vals[s, h, HEAD_DIM:VROWS] = jnp.ones((VROWS - HEAD_DIM, T), BF16)
    project(0, features)
    make_bias(0)

    def score(slot, pair, h, t, a, fresh):
        best = None
        for kc in range(2):
            ks = slice(kc * 256, (kc + 1) * 256)
            s = mm(keys[slot, pair, ks], qz[h]) + bias[slot, ks]
            t[ks] = s
            m = jnp.max(s, axis=0, keepdims=True)
            best = m if best is None else jnp.maximum(best, m)
        if fresh:
            top[h] = jnp.broadcast_to(best, (8, T))
        else:
            old = top[h]
            new = jnp.maximum(old, best)
            a[...] = jnp.exp2((old - new) * SCALE)
            top[h] = new

    def weigh(h, t, p):
        m = top[h][0:1]
        for kc in range(4):
            ks = slice(kc * 128, (kc + 1) * 128)
            p[ks] = jnp.exp2((t[ks] - m) * SCALE).astype(BF16)

    def gather(slot, h, p, a, fresh):
        new = mm(vals[slot, h], p[...])[0:AROWS]
        if fresh:
            acc[h] = new
        else:
            acc[h] = acc[h] * a[0:1] + new

    def attend(slot, fresh=False):
        score(slot, 0, 0, t0, a0, fresh)
        score(slot, 0, 1, t1, a1, fresh)
        weigh(0, t0, p0)

        def step(j, carry):
            gather(slot, 2 * j - 2, p0, a0, fresh)
            weigh(2 * j - 1, t1, p1)
            score(slot, j, 2 * j, t0, a0, fresh)
            gather(slot, 2 * j - 1, p1, a1, fresh)
            weigh(2 * j, t0, p0)
            score(slot, j, 2 * j + 1, t1, a1, fresh)
            return carry

        lax.fori_loop(1, HEADS // 2, step, 0)
        weigh(HEADS - 1, t1, p1)
        gather(slot, HEADS - 2, p0, a0, fresh)
        gather(slot, HEADS - 1, p1, a1, fresh)

    attend(0, fresh=True)

    for copy in first:
        copy.wait_send()
    for copy in second:
        copy.start()
    first[0].wait_recv()
    passed[0].start()

    own.wait_recv()
    project(1, recv[0])
    make_bias(1)
    attend(1)

    for copy in first[1:]:
        copy.wait_recv()
    for copy in passed[1:]:
        copy.start()
    project(2, recv[1])
    make_bias(2)
    attend(2)

    for copy in passed:
        copy.wait_recv()
    project(3, recv[2])
    make_bias(3)
    attend(3)

    for copy in second:
        copy.wait_recv()
    project(4, recv[3])
    make_bias(4)
    attend(4)

    for h in range(HEADS):
        a = acc[h]
        mixed[h * HEAD_DIM : (h + 1) * HEAD_DIM] = (
            a[0:HEAD_DIM] / a[HEAD_DIM : HEAD_DIM + 1]
        ).astype(BF16)
    for copy in late:
        copy.wait()
    mix = mixed[...].T
    res = atoms[...].astype(F32) + mm(mix, wo[...])
    after[...] = res

    mean = jnp.sum(res, axis=0, keepdims=True) * (1.0 / T)
    dev = after[...] - mean
    m2 = jnp.sum(dev * dev, axis=0, keepdims=True)
    stat[0:1] = mean
    stat[1:2] = m2

    def merge(mean, m2, others, count, size):
        total = mean
        for j in range(1, count):
            total = total + others[j, 0:1]
        new = total * (1.0 / count)
        spread = (mean - new) * (mean - new)
        for j in range(1, count):
            d = others[j, 0:1] - new
            spread = spread + d * d
            m2 = m2 + others[j, 1:2]
        return new, m2 + spread * size

    plane = [
        remote(stat, stat_a.at[j], sa_send.at[j], sa_recv.at[j], plane_peer(j))
        for j in range(1, PLANE)
    ]
    for copy in plane:
        copy.start()
    for copy in plane:
        copy.wait_recv()
    mean, m2 = merge(mean, m2, stat_a, PLANE, float(T))
    stat_m[0:1] = mean
    stat_m[1:2] = m2
    line = [
        remote(stat_m, stat_b.at[j], sb_send.at[j], sb_recv.at[j], line_peer(j))
        for j in range(1, NZ)
    ]
    for copy in line:
        copy.start()
    for copy in line:
        copy.wait_recv()
    mean, m2 = merge(mean, m2, stat_b, NZ, float(T * PLANE))
    var = m2 * (1.0 / (T * BLOCKS))
    factor = lax.rsqrt(var + 1e-5) * bng[...]

    outs = []
    for c in range(2):
        rs = slice(c * 256, (c + 1) * 256)
        a = after[rs]
        batched = ((a - mean) * factor + bns[...]).astype(BF16)
        hidden = jax.nn.gelu(mm(batched, wu[...]), approximate=True).astype(BF16)
        result[rs] = (a + mm(hidden, wd[...])).astype(BF16)
        copy = pltpu.make_async_copy(result.at[rs], out_hbm.at[rs], out_sem.at[c])
        copy.start()
        outs.append(copy)

    own.wait_send()
    for copy in passed + second + plane + line:
        copy.wait_send()
    for copy in outs:
        copy.wait()


def body(atoms, edge_mask, norm_gain, w_query, w_key, w_value, w_out, bn_gain, bn_shift, w_up, w_down):
    dma = pltpu.SemaphoreType.DMA
    args = (
        atoms, edge_mask, norm_gain.reshape(1, D), w_query, w_key, w_value, w_out,
        bn_gain.reshape(1, D), bn_shift.reshape(1, D), w_up, w_down,
    )
    vm = pltpu.VMEM
    return pl.pallas_call(
        kernel,
        out_shape=jax.ShapeDtypeStruct((T, D), BF16),
        in_specs=[pl.BlockSpec(memory_space=pl.ANY)] * len(args),
        out_specs=pl.BlockSpec(memory_space=pl.ANY),
        scratch_shapes=[
            vm((T, D), BF16), vm((SLABS, T, T), jnp.int32), vm((1, D), F32),
            vm((D, D), BF16), vm((D, D), BF16), vm((D, D), BF16), vm((D, D), BF16),
            vm((1, D), F32), vm((1, D), F32), vm((D, FF), BF16), vm((FF, D), BF16),
            vm((T, D), BF16), vm((4, T, D), BF16), vm((D, D), BF16), vm((D, D), BF16),
            vm((HEADS, 2 * HEAD_DIM, T), BF16), vm((SLABS, HEADS // 2, T, 128), BF16),
            vm((SLABS, HEADS, VROWS, T), BF16), vm((SLABS, T, T), F32),
            vm((T, T), F32), vm((T, T), F32), vm((T, T), BF16), vm((T, T), BF16),
            vm((8, T), F32), vm((8, T), F32), vm((HEADS, 8, T), F32), vm((HEADS, AROWS, T), F32),
            vm((D, T), BF16), vm((T, D), F32), vm((T, D), BF16),
            vm((2, D), F32), vm((PLANE, 2, D), F32), vm((2, D), F32), vm((NZ, 2, D), F32),
            dma((15,)), dma((2,)), dma, dma, dma((CHUNKS,)), dma((CHUNKS,)),
            dma((CHUNKS,)), dma((CHUNKS,)), dma((CHUNKS,)), dma((CHUNKS,)),
            dma((PLANE,)), dma((PLANE,)), dma((NZ,)), dma((NZ,)),
        ],
        compiler_params=pltpu.CompilerParams(
            collective_id=0, has_side_effects=True, vmem_limit_bytes=63000 * 1024
        ),
    )(*args)


def solution(mesh):
    rows = P(("grp", "blk"), None)
    return jax.shard_map(
        body,
        mesh=mesh,
        in_specs=(rows, P(("grp", "blk"), None, None, None)) + (P(),) * 9,
        out_specs=rows,
        check_vma=False,
    )
```

time: 127 us -> 48.8 us (0.38)
  matrix products: 52 us -> 0 us
  Pallas kernels: 0 us -> 46.8 us
  blocking collectives: 37.9 us -> 0 us
  other arithmetic: 18.7 us -> 0 us
  starting transfers between devices: 12.4 us -> 0 us
  local copies, waits for them, and re-layouts: 5.27 us -> 1.87 us
    dot_general x23 -> x0, matrix products: 52 us -> none  [the longest x5 15.4 us: attend_block(): jnp.einsum('hqk,khd->qhd', expo.astype(jnp.bfloat16), value_heads, prefer...]
    pallas_call x0 -> x1, Pallas kernels: none -> 46.8 us  [body(): pl.pallas_call(kernel, out_shape=jax.ShapeDtypeStruct((T, D), BF16), in_s...]
    psum x4 -> x0, blocking collectives: 37.9 us -> none  [one_axis_at_a_time(): value = lax.psum(value, axis)]
    reduce_sum x4 -> x0, other arithmetic: 15.5 us -> none  [the longest x3 14.1 us: attend_block(): new_total = running_total * factor + jnp.sum(expo, axis=-1)]
    ppermute x4 -> x0, starting transfers between devices: 12.4 us -> none  [passed_along(): return lax.ppermute(value, axis, pairs)]
    gt x4 -> x0, local copies, waits for them, and re-layouts: 4.14 us -> none  [body(): masks[offset + REACH] > 0]
    unnamed x30 -> x1, local copies, waits for them, and re-layouts: 0.08 us -> 1.87 us
    convert_element_type x1 -> x0, other arithmetic: 1.65 us -> none  [body(): normed = (xfull * lax.rsqrt(jnp.mean(xfull * xfull, axis=-1, keepdims=Tru...]
  transfers between devices with their start and end apart: 4 -> 0, of which waited for: 0 -> 0; matrix products, arithmetic and copies ran while one was open for 22% -> 0% of each run, Pallas kernels for 0% -> 0%
where the time goes in v1:
time: 48.8 us; the launch traced here: 48.6 us
  Pallas kernels  46.8 us (96%)
  local copies, waits for them, and re-layouts  1.87 us (4%)
    pallas_call x1, Pallas kernels, body(): pl.pallas_call(kernel, out_shape=jax.ShapeDtypeStruct((T, D), BF16), in_s...  46.8 us
    unnamed x1, local copies, waits for them, and re-layouts  1.87 us

profile of v1, /device:TPU:1, one launch (start us, length us, event | category | flops | bytes accessed | tf_op | source)
XLA Modules:
  0.0 48.6 jit_solution(18438618699000995007)
XLA Ops:
  0.0 46.8 %shard_map.109 = bf16[512,512]{1,0:T(8,128)(2,1)} custom-call(bf16[512,512]{1,0:T(8,128)(2,1)} %atoms_hbm.1, s32[1,5,512,512]{3,2,1,0:T(8,128)} %mask_hbm.1, f32[1,512]{1,0:T(1,128)} %bitcast.3, bf16[512,512]{1,0:T(8,128)(2,1)} %wq_hbm.1, bf16[512,512]{1,0:T(8,128)(2,1)} %wk_hbm.1, bf16[512,512]{1,0:T(8,128)(2,1)} %wv_hbm.1, bf16[512,512]{1,0:T(8,128)(2,1)} %wo_hbm.1, ...), custom_call_target="tpu_custom_call" | custom-call | tf_op jit(solution)/shard_map/pallas_call | solution.py:325
  46.8 1.9 %copy.13 = bf16[512,512]{1,0:T(8,128)(2,1)} copy(bf16[512,512]{1,0:T(8,128)(2,1)} %shard_map.109) | data formatting | bytes 1048576

commit v2 on v1

--- a/solution.py
+++ b/solution.py
@@ -39,7 +39,7 @@
     atoms_hbm, mask_hbm, gain_hbm, wq_hbm, wk_hbm, wv_hbm, wo_hbm, bng_hbm, bns_hbm, wu_hbm, wd_hbm,
     out_hbm,
     atoms, mask, gain, wq, wk, wv, wo, bng, bns, wu, wd,
-    nrm, recv, wqt, wvt, qz, keys, vals, bias, t0, t1, p0, p1, a0, a1, top, acc,
+    nrm, recv, wqt, wvt, qz, keys, vals, bias, t0, t1, a0, a1, top, acc,
     mixed, after, result, stat, stat_a, stat_m, stat_b,
     load_sem, out_sem, own_send, own_recv, fst_send, fst_recv, fwd_send, fwd_recv, snd_send, snd_recv,
     sa_send, sa_recv, sb_send, sb_recv,
@@ -116,19 +116,22 @@
         for c in range(CHUNKS)
     ]
 
-    loads[0].wait()
-    loads[1].wait()
+    with jax.named_scope("w_atoms"):
+        loads[0].wait()
+        loads[1].wait()
     x = atoms[...].astype(F32)
     nrm[...] = (
         x * lax.rsqrt(jnp.mean(x * x, axis=-1, keepdims=True) + 1e-6) * gain[...]
     ).astype(BF16)
-    pl.semaphore_wait(barrier, len(peers))
+    with jax.named_scope("w_barrier"):
+        pl.semaphore_wait(barrier, len(peers))
     for copy in first:
         copy.start()
     own.start()
 
-    for copy in loads[2:]:
-        copy.wait()
+    with jax.named_scope("w_weights"):
+        for copy in loads[2:]:
+            copy.wait()
     wqt[...] = wq[...].T
     wvt[...] = wv[...].T
 
@@ -151,23 +154,29 @@
             bias[slot, kc * 128 : (kc + 1) * 128] = jnp.where(allowed, 0.0, NEG).astype(F32).T
 
     features = nrm[...]
-    q = mm_nt(wqt[...], features).astype(BF16)
+    q = mm_nt(wqt[...], features).astype(BF16).astype(F32) * SCALE
+    high = q.astype(BF16)
+    low = (q - high.astype(F32)).astype(BF16)
     zero = jnp.zeros((HEAD_DIM, T), BF16)
     for h in range(HEADS):
-        part = q[h * HEAD_DIM : (h + 1) * HEAD_DIM]
-        qz[h, 0:HEAD_DIM] = part if h % 2 == 0 else zero
-        qz[h, HEAD_DIM : 2 * HEAD_DIM] = zero if h % 2 == 0 else part
+        for i, piece in enumerate((high, low)):
+            part = piece[h * HEAD_DIM : (h + 1) * HEAD_DIM]
+            at = i * 2 * HEAD_DIM
+            qz[h, at : at + HEAD_DIM] = part if h % 2 == 0 else zero
+            qz[h, at + HEAD_DIM : at + 2 * HEAD_DIM] = zero if h % 2 == 0 else part
     for s in range(SLABS):
         for h in range(HEADS):
             vals[s, h, HEAD_DIM:VROWS] = jnp.ones((VROWS - HEAD_DIM, T), BF16)
     project(0, features)
     make_bias(0)
 
-    def score(slot, pair, h, t, a, fresh):
+    def score(slot, h, fresh):
+        t, a = (t0, a0) if h % 2 == 0 else (t1, a1)
         best = None
         for kc in range(2):
             ks = slice(kc * 256, (kc + 1) * 256)
-            s = mm(keys[slot, pair, ks], qz[h]) + bias[slot, ks]
+            kp = keys[slot, h // 2, ks]
+            s = mm(jnp.concatenate([kp, kp], axis=1), qz[h]) + bias[slot, ks]
             t[ks] = s
             m = jnp.max(s, axis=0, keepdims=True)
             best = m if best is None else jnp.maximum(best, m)
@@ -176,79 +185,68 @@
         else:
             old = top[h]
             new = jnp.maximum(old, best)
-            a[...] = jnp.exp2((old - new) * SCALE)
+            a[...] = jnp.exp2(old - new)
             top[h] = new
 
-    def weigh(h, t, p):
-        m = top[h][0:1]
-        for kc in range(4):
-            ks = slice(kc * 128, (kc + 1) * 128)
-            p[ks] = jnp.exp2((t[ks] - m) * SCALE).astype(BF16)
-
-    def gather(slot, h, p, a, fresh):
-        new = mm(vals[slot, h], p[...])[0:AROWS]
-        if fresh:
-            acc[h] = new
-        else:
-            acc[h] = acc[h] * a[0:1] + new
+    def gather(slot, h, fresh):
+        t, a = (t0, a0) if h % 2 == 0 else (t1, a1)
+        for qc in range(2):
+            qs = slice(qc * 256, (qc + 1) * 256)
+            m = top[h, 0:1, qs]
+            p = jnp.exp2(t[:, qs] - m).astype(BF16)
+            new = mm(vals[slot, h], p)[0:AROWS]
+            if fresh:
+                acc[h, :, qs] = new
+            else:
+                acc[h, :, qs] = acc[h, :, qs] * a[0:1, qs] + new
 
     def attend(slot, fresh=False):
-        score(slot, 0, 0, t0, a0, fresh)
-        score(slot, 0, 1, t1, a1, fresh)
-        weigh(0, t0, p0)
-
-        def step(j, carry):
-            gather(slot, 2 * j - 2, p0, a0, fresh)
-            weigh(2 * j - 1, t1, p1)
-            score(slot, j, 2 * j, t0, a0, fresh)
-            gather(slot, 2 * j - 1, p1, a1, fresh)
-            weigh(2 * j, t0, p0)
-            score(slot, j, 2 * j + 1, t1, a1, fresh)
-            return carry
-
-        lax.fori_loop(1, HEADS // 2, step, 0)
-        weigh(HEADS - 1, t1, p1)
-        gather(slot, HEADS - 2, p0, a0, fresh)
-        gather(slot, HEADS - 1, p1, a1, fresh)
-
-    attend(0, fresh=True)
-
-    for copy in first:
-        copy.wait_send()
+        score(slot, 0, fresh)
+        for h in range(HEADS):
+            if h + 1 < HEADS:
+                score(slot, h + 1, fresh)
+            gather(slot, h, fresh)
+
+    with jax.named_scope("w_partner"):
+        own.wait_recv()
+    with jax.named_scope("attend0"):
+        project(1, recv[0])
+        attend(0, fresh=True)
+        make_bias(1)
     for copy in second:
         copy.start()
-    first[0].wait_recv()
+    with jax.named_scope("attend1"):
+        attend(1)
+    with jax.named_scope("w_first0"):
+        first[0].wait_recv()
     passed[0].start()
-
-    own.wait_recv()
-    project(1, recv[0])
-    make_bias(1)
-    attend(1)
-
-    for copy in first[1:]:
-        copy.wait_recv()
+    for s in range(2, SLABS):
+        make_bias(s)
+    with jax.named_scope("w_first1"):
+        for copy in first[1:]:
+            copy.wait_recv()
     for copy in passed[1:]:
         copy.start()
-    project(2, recv[1])
-    make_bias(2)
-    attend(2)
-
-    for copy in passed:
-        copy.wait_recv()
-    project(3, recv[2])
-    make_bias(3)
-    attend(3)
-
-    for copy in second:
-        copy.wait_recv()
-    project(4, recv[3])
-    make_bias(4)
-    attend(4)
+    with jax.named_scope("attend2"):
+        project(2, recv[1])
+        attend(2)
+    with jax.named_scope("w_passed"):
+        for copy in passed:
+            copy.wait_recv()
+    with jax.named_scope("attend3"):
+        project(3, recv[2])
+        attend(3)
+    with jax.named_scope("w_second"):
+        for copy in second:
+            copy.wait_recv()
+    with jax.named_scope("attend4"):
+        project(4, recv[3])
+        attend(4)
 
     for h in range(HEADS):
         a = acc[h]
         mixed[h * HEAD_DIM : (h + 1) * HEAD_DIM] = (
-            a[0:HEAD_DIM] / a[HEAD_DIM : HEAD_DIM + 1]
+            a[0:HEAD_DIM] * (1.0 / a[HEAD_DIM : HEAD_DIM + 1])
         ).astype(BF16)
     for copy in late:
         copy.wait()
@@ -280,8 +278,9 @@
     ]
     for copy in plane:
         copy.start()
-    for copy in plane:
-        copy.wait_recv()
+    with jax.named_scope("w_plane"):
+        for copy in plane:
+            copy.wait_recv()
     mean, m2 = merge(mean, m2, stat_a, PLANE, float(T))
     stat_m[0:1] = mean
     stat_m[1:2] = m2
@@ -291,8 +290,9 @@
     ]
     for copy in line:
         copy.start()
-    for copy in line:
-        copy.wait_recv()
+    with jax.named_scope("w_line"):
+        for copy in line:
+            copy.wait_recv()
     mean, m2 = merge(mean, m2, stat_b, NZ, float(T * PLANE))
     var = m2 * (1.0 / (T * BLOCKS))
     factor = lax.rsqrt(var + 1e-5) * bng[...]
@@ -309,10 +309,11 @@
         outs.append(copy)
 
     own.wait_send()
-    for copy in passed + second + plane + line:
+    for copy in first + passed + second + plane + line:
         copy.wait_send()
-    for copy in outs:
-        copy.wait()
+    with jax.named_scope("w_outs"):
+        for copy in outs:
+            copy.wait()
 
 
 def body(atoms, edge_mask, norm_gain, w_query, w_key, w_value, w_out, bn_gain, bn_shift, w_up, w_down):
@@ -332,9 +333,9 @@
             vm((D, D), BF16), vm((D, D), BF16), vm((D, D), BF16), vm((D, D), BF16),
             vm((1, D), F32), vm((1, D), F32), vm((D, FF), BF16), vm((FF, D), BF16),
             vm((T, D), BF16), vm((4, T, D), BF16), vm((D, D), BF16), vm((D, D), BF16),
-            vm((HEADS, 2 * HEAD_DIM, T), BF16), vm((SLABS, HEADS // 2, T, 128), BF16),
+            vm((HEADS, 4 * HEAD_DIM, T), BF16), vm((SLABS, HEADS // 2, T, 128), BF16),
             vm((SLABS, HEADS, VROWS, T), BF16), vm((SLABS, T, T), F32),
-            vm((T, T), F32), vm((T, T), F32), vm((T, T), BF16), vm((T, T), BF16),
+            vm((T, T), F32), vm((T, T), F32),
             vm((8, T), F32), vm((8, T), F32), vm((HEADS, 8, T), F32), vm((HEADS, AROWS, T), F32),
             vm((D, T), BF16), vm((T, D), F32), vm((T, D), BF16),
             vm((2, D), F32), vm((PLANE, 2, D), F32), vm((2, D), F32), vm((NZ, 2, D), F32),

time: 48.8 us -> 46.4 us (0.951)
  Pallas kernels: 46.8 us -> 44.4 us
    pallas_call x1, Pallas kernels: 46.8 us -> 44.4 us  [body(): pl.pallas_call(kernel, out_shape=jax.ShapeDtypeStruct((T, D), BF16), in_s...]
where the time goes in v2:
time: 46.4 us; the launch traced here: 46.3 us
  Pallas kernels  44.4 us (96%)
  local copies, waits for them, and re-layouts  1.87 us (4%)
    pallas_call x1, Pallas kernels, body(): pl.pallas_call(kernel, out_shape=jax.ShapeDtypeStruct((T, D), BF16), in_s...  44.4 us
    unnamed x1, local copies, waits for them, and re-layouts  1.87 us

profile of v2, /device:TPU:1, one launch (start us, length us, event | category | flops | bytes accessed | tf_op | source)
XLA Modules:
  0.0 46.3 jit_solution(6936592927166946937)
XLA Ops:
  0.0 44.4 %shard_map.109 = bf16[512,512]{1,0:T(8,128)(2,1)} custom-call(bf16[512,512]{1,0:T(8,128)(2,1)} %atoms_hbm.1, s32[1,5,512,512]{3,2,1,0:T(8,128)} %mask_hbm.1, f32[1,512]{1,0:T(1,128)} %bitcast.3, bf16[512,512]{1,0:T(8,128)(2,1)} %wq_hbm.1, bf16[512,512]{1,0:T(8,128)(2,1)} %wk_hbm.1, bf16[512,512]{1,0:T(8,128)(2,1)} %wv_hbm.1, bf16[512,512]{1,0:T(8,128)(2,1)} %wo_hbm.1, ...), custom_call_target="tpu_custom_call" | custom-call | tf_op jit(solution)/shard_map/pallas_call | solution.py:326
  44.4 1.9 %copy.13 = bf16[512,512]{1,0:T(8,128)(2,1)} copy(bf16[512,512]{1,0:T(8,128)(2,1)} %shard_map.109) | data formatting | bytes 1048576
